TPU v7x, 32 devices: a whole 2x2x4 slice. The times are simulated.
32 devices in a mesh: mem: 8 (over z, x), geo: 4 (over y, core).
Axes of the slice: x: 2, y: 2, z: 4, core: 2. Of those that a mesh axis runs over, the one named last changes fastest.
Arguments:
- control: float32 [8, 32, 48, 384], P('mem', 'geo'), may hold values from -6 to 6
- kappa_table: float32 [16], replicated, may hold values from 0.02 to 0.24
- kappa_index: int32 [48, 384], replicated, may hold values from 0 to 15
- tile_bounds: int32 [5], replicated, may hold values from 0 to 18432, as said below
- filter_bands: float32 [4, 5, 32], replicated, may hold values from -0.3 to 0.3
- perturbation: bfloat16 [2, 8, 32, 18432], P(None, 'mem', None, 'geo'), may hold values from -6 to 6
Outputs:
- increment: float32 [2, 32, 18432], P(None, 'mem', 'geo')
Inputs may be any that keep to these rules, and one draw needn't show every extreme that they name: tile_bounds[0] is 0, tile_bounds[4] is 18432, and the bounds never fall; tile t holds columns tile_bounds[t] to tile_bounds[t + 1] - 1.
All inputs are finite; a program needn't handle non-finite values.
Results may differ from a plain program's by a relative error of at most 0.005.
Values may be sent and summed in bfloat16 or wider, within the bound.
A program may use at most 64 MiB of HBM per device.

v0:
```python
import functools

import jax
import jax.numpy as jnp
from jax import lax
from jax.experimental import pallas as pl
from jax.experimental.pallas import tpu as pltpu
from jax.sharding import PartitionSpec as P

ITERS = 10
F32, BF16 = jnp.float32, jnp.bfloat16
LANES = 128


def inner_size(nm):
    q = 1
    while nm % (2 * q) == 0 and (2 * q) ** 2 <= 2 * nm:
        q *= 2
    return q


def kernel(nm, ng, q, ctrl, table_hbm, kidx_hbm, bounds_hbm, bands_hbm, pert_hbm, out,
           table, bounds, C, S, WE, WN, FL, spread, gather, kidx, kf, bands, bandsb, coef, pert,
           PS, PR, B, G, D, FS, FR, XS, XR, OWN, YS, YR,
           loc_sem, ps_sem, pr_sem, gs_sem, gr_sem, as_sem, ar_sem, bs_sem, br_sem):
    mem = lax.axis_index("mem")
    geo = lax.axis_index("geo")
    o = nm // q
    inner = lax.rem(mem, q)
    outer = mem // q
    hx, lev, hy = S.shape
    nvar, levels, cols = pert.shape
    lm = levels // nm
    wide = levels // q
    rows = hx // ng
    nband, tiles, _ = bands.shape
    parts = hy // LANES
    pad = nband // 2
    nc = FS.shape[1]
    cr = rows // nc
    cw = cr * hy
    npc = XS.shape[1]
    backward = geo < ng // 2

    def at_inner(d):
        return {"mem": outer * q + lax.rem(inner + d, q)}

    def at_outer(d):
        return {"mem": lax.rem(outer + d, o) * q + inner}

    barrier = pltpu.get_barrier_semaphore()
    targets = ([at_inner(d) for d in range(1, q)] + [at_outer(d) for d in range(1, o)]
               + [{"geo": lax.rem(geo + d, ng)} for d in range(1, ng)])
    for target in targets:
        pl.semaphore_signal(barrier, inc=1, device_id=target, device_id_type=pl.DeviceIdType.MESH)

    kidx_cp = pltpu.make_async_copy(kidx_hbm, kidx, loc_sem.at[1])
    kidx_cp.start()
    table_cp = pltpu.make_async_copy(table_hbm, table, loc_sem.at[3])
    table_cp.start()
    pert_cp = pltpu.make_async_copy(pert_hbm.at[:, 0], pert, loc_sem.at[0])
    pert_cp.start()
    ctrl_cps = []
    for l in range(lev):
        cp = pltpu.make_async_copy(ctrl.at[0, l], C.at[:, l], loc_sem.at[5 + l])
        cp.start()
        ctrl_cps.append(cp)
    bands_cp = pltpu.make_async_copy(bands_hbm, bands, loc_sem.at[2])
    bands_cp.start()
    bounds_cp = pltpu.make_async_copy(bounds_hbm, bounds, loc_sem.at[4])
    bounds_cp.start()

    left = lax.broadcasted_iota(jnp.int32, (hy, hy), 0)
    right = lax.broadcasted_iota(jnp.int32, (hy, hy), 1)
    spread[...] = jnp.where(left == (right % LANES) * parts + right // LANES, 1.0, 0.0).astype(BF16)
    gather[...] = jnp.where(right == (left % LANES) * parts + left // LANES, 1.0, 0.0).astype(BF16)

    def turned(i, last):
        return jnp.where(backward, last - i, i)

    kidx_cp.wait()
    table_cp.wait()
    index = jnp.dot(kidx[...].astype(F32).astype(BF16), spread[...], preferred_element_type=F32)
    field = jnp.zeros(index.shape, F32)
    for entry in range(table.shape[0]):
        field = jnp.where(index == float(entry), table[entry], field)
    kf[0:hx] = field
    kf[hx:] = jnp.zeros((kf.shape[0] - hx, hy), F32)
    east = 0.5 * (field + kf[1:hx + 1])
    lane = lax.broadcasted_iota(jnp.int32, (hx, LANES), 1)
    cut = [field[:, p * LANES:(p + 1) * LANES] for p in range(parts)]
    norths = [0.5 * (cut[p] + cut[p + 1]) for p in range(parts - 1)]
    last = 0.5 * (cut[-1] + pltpu.roll(cut[0], LANES - 1, axis=1))
    norths.append(jnp.where(lane < LANES - 1, last, 0.0))
    for i in range(hx):
        if i < hx - 1:
            WE[turned(i, hx - 2)] = jnp.broadcast_to(east[i:i + 1], (lev, hy))
        to = turned(i, hx - 1)
        for p in range(parts):
            WN[to, :, p * LANES:(p + 1) * LANES] = jnp.broadcast_to(norths[p][i:i + 1], (lev, LANES))

    def piece(vals, i):
        return jnp.concatenate([v[(k * q + i) * lm:(k * q + i + 1) * lm] for v in vals for k in range(o)], axis=0)

    def strip(k):
        return pl.ds(pl.multiple_of(k * hy, LANES), hy)

    pert_cp.wait()
    for c in range(npc, nc):
        def repack(r, carry, c=c):
            at = strip(c * cr + r)
            vals = [pert[v, :, at].astype(F32) for v in range(nvar)]
            for i in range(q):
                PS[i, c - npc, :, strip(r)] = piece(vals, i).astype(BF16)
            return carry

        lax.fori_loop(0, cr, repack, 0)
    pl.semaphore_wait(barrier, len(targets))

    def inner_copy(src, dst, send, recv, c, k, d):
        return pltpu.make_async_remote_copy(
            src_ref=src.at[lax.rem(inner + d, q), k], dst_ref=dst.at[d, k], send_sem=send.at[d, c], recv_sem=recv.at[d, c],
            device_id=at_inner(d), device_id_type=pl.DeviceIdType.MESH)

    pert_ex = [[inner_copy(PS, PR, ps_sem, pr_sem, c, c - npc, d) for d in range(1, q)] for c in range(npc, nc)]
    for cps in pert_ex:
        for cp in cps:
            cp.start()

    for cp in ctrl_cps:
        cp.wait()
    group = rows if (rows * lev) % 8 == 0 else hx
    for i in range(0, hx, group):
        x = C[i:i + group].reshape(group * lev, hy)
        high = x.astype(BF16)
        low = (x - high.astype(F32)).astype(BF16)
        x = (jnp.dot(high, spread[...], preferred_element_type=F32)
             + jnp.dot(low, spread[...], preferred_element_type=F32))
        x = x.reshape(group, lev, hy)
        for r in range(group):
            S[turned(i + r, hx - 1)] = x[r]

    def row_of(ref, i):
        return [ref[i, :, p * LANES:(p + 1) * LANES] for p in range(parts)]

    def sweep(it, lo, count, first, final):
        s = row_of(S, lo)
        before = None if first else row_of(FL, it)
        for j in range(count):
            i = lo + j
            wn = row_of(WN, i)
            ahead = s[1:] + [pltpu.roll(s[0], LANES - 1, axis=1)]
            flux = [wn[p] * (ahead[p] - s[p]) for p in range(parts)]
            behind = [pltpu.roll(flux[-1], 1, axis=1)] + flux[:-1]
            new = [s[p] + (flux[p] - behind[p]) for p in range(parts)]
            if before is not None:
                new = [new[p] - before[p] for p in range(parts)]
            if not (final and j == count - 1):
                after = row_of(S, i + 1)
                we = row_of(WE, i)
                before = [we[p] * (after[p] - s[p]) for p in range(parts)]
                new = [new[p] + before[p] for p in range(parts)]
                s = after
            for p in range(parts):
                S[i, :, p * LANES:(p + 1) * LANES] = new[p]
        if not final:
            for p in range(parts):
                FL[it, :, p * LANES:(p + 1) * LANES] = before[p]

    geo_all = []
    for b in range(ng):
        for it in range(ITERS):
            ahead = ITERS - 1 - it
            lo = 0 if b == 0 else min(hx, rows * b + ahead)
            hi = min(hx, rows * (b + 1) + ahead)
            if hi > lo:
                sweep(it, lo, hi - lo, lo == 0, hi == hx)
        band = turned(b, ng - 1)
        if (rows * lev) % 8 == 0:
            x = S[b * rows:(b + 1) * rows].reshape(rows * lev, hy).astype(BF16)
            x = jnp.dot(x, gather[...], preferred_element_type=F32).reshape(rows, lev, hy).astype(BF16)
        else:
            x = [jnp.dot(S[b * rows + r].astype(BF16), gather[...], preferred_element_type=F32).astype(BF16)
                 for r in range(rows)]
        for r in range(rows):
            B[turned(b * rows + r, hx - 1)] = x[r]
        d = lax.rem(band - geo + ng, ng)
        cps = [pltpu.make_async_remote_copy(
            src_ref=B.at[pl.ds(band * rows + c * cr, cr)], dst_ref=G.at[geo, pl.ds(c * cr, cr)],
            send_sem=gs_sem.at[b, c], recv_sem=gr_sem.at[d, c],
            device_id={"geo": band}, device_id_type=pl.DeviceIdType.MESH) for c in range(nc)]
        geo_all.append((band, cps))
        if b < ng // 2:
            for cp in cps:
                cp.start()
        else:
            @pl.when(band != geo)
            def _(cps=cps):
                for cp in cps:
                    cp.start()

    own_geo = [pltpu.make_async_copy(B.at[pl.ds(geo * rows + c * cr, cr)], G.at[geo, pl.ds(c * cr, cr)], gr_sem.at[0, c])
               for c in range(nc)]
    for cp in own_geo:
        cp.start()

    bands_cp.wait()
    bounds_cp.wait()
    eye = (lax.broadcasted_iota(jnp.int32, (levels, levels), 0)
           == lax.broadcasted_iota(jnp.int32, (levels, levels), 1))
    for t in range(tiles):
        for k in range(nband):
            row = jnp.broadcast_to(bands[k, t:t + 1, :], (levels, levels))
            column = jnp.sum(jnp.where(eye, row, 0.0), axis=1, keepdims=True)
            bandsb[t, k] = jnp.broadcast_to(column, (levels, LANES))

    def coefficients(k, carry):
        at = pl.ds(pl.multiple_of(k * LANES, LANES), LANES)
        column = geo * cols + k * LANES + lax.broadcasted_iota(jnp.int32, (levels, LANES), 1)
        past = [column >= bounds[t] for t in range(1, tiles)]
        for k in range(nband):
            value = bandsb[0, k]
            for t in range(1, tiles):
                value = jnp.where(past[t - 1], bandsb[t, k], value)
            coef[k, :, at] = value
        return carry

    lax.fori_loop(0, cols // LANES, coefficients, 0)
    base = 8
    D[0:base, :] = jnp.zeros((base, cols), F32)
    D[base + levels:, :] = jnp.zeros((D.shape[0] - base - levels, cols), F32)

    def filtered(k):
        at = strip(k)
        value = D[base:base + levels, at]
        for n in range(nband):
            value = value + coef[n, :, at] * D[base + n - pad:base + n - pad + levels, at]
        return value.astype(BF16).astype(F32), at

    def arrived(d, c):
        return pltpu.make_async_remote_copy(
            src_ref=B.at[pl.ds(c * cr, cr)], dst_ref=G.at[0, pl.ds(c * cr, cr)],
            send_sem=gs_sem.at[0, c], recv_sem=gr_sem.at[d, c],
            device_id={"geo": lax.rem(geo + d, ng)}, device_id_type=pl.DeviceIdType.MESH)

    filt_ex = []
    for c in range(nc):
        own_geo[c].wait()
        for d in range(1, ng):
            arrived(d, c).wait_recv()

        def vertical(r, carry, c=c):
            k = c * cr + r
            for g in range(ng):
                D[base + g * lev:base + (g + 1) * lev, strip(k)] = G[g, k].astype(F32)
            value, at = filtered(k)
            if c < npc:
                vals = [pert[v, :, at].astype(F32) * value for v in range(nvar)]
                for i in range(q):
                    XS[i, c, :, strip(r)] = piece(vals, i).astype(BF16)
            else:
                for i in range(q):
                    FS[i, c, :, strip(r)] = piece([value], i).astype(BF16)
            return carry

        lax.fori_loop(0, cr, vertical, 0)
        if c < npc:
            cps = [inner_copy(XS, XR, as_sem, ar_sem, c, c, d) for d in range(1, q)]
        else:
            cps = [inner_copy(FS, FR, as_sem, ar_sem, c, c, d) for d in range(1, q)]
        for cp in cps:
            cp.start()
        filt_ex.append(cps)

    outer_ex = []
    for c in range(nc):
        for cp in filt_ex[c]:
            cp.wait_recv()
        if c >= npc:
            for cp in pert_ex[c - npc]:
                cp.wait_recv()

        def total(r, carry, c=c):
            at = strip(r)
            if c < npc:
                acc = XS[inner, c, :, at].astype(F32)
                for d in range(1, q):
                    acc = acc + XR[d, c, :, at].astype(F32)
            else:
                f = FS[inner, c, :, at].astype(F32)
                acc = PS[inner, c - npc, :, at].astype(F32) * jnp.concatenate([f] * nvar, axis=0)
                for d in range(1, q):
                    f = FR[d, c, :, at].astype(F32)
                    acc = acc + PR[d, c - npc, :, at].astype(F32) * jnp.concatenate([f] * nvar, axis=0)
            shares = [jnp.concatenate([acc[v * wide + k * lm:v * wide + (k + 1) * lm] for v in range(nvar)], axis=0)
                      for k in range(o)]
            mine = shares[0]
            for k in range(o):
                YS[k, c, :, at] = shares[k].astype(BF16)
                if k:
                    mine = jnp.where(outer == k, shares[k], mine)
            OWN[c, :, at] = mine
            return carry

        lax.fori_loop(0, cr, total, 0)
        cps = [pltpu.make_async_remote_copy(
            src_ref=YS.at[lax.rem(outer + d, o), c], dst_ref=YR.at[d, c], send_sem=bs_sem.at[d, c], recv_sem=br_sem.at[d, c],
            device_id=at_outer(d), device_id_type=pl.DeviceIdType.MESH) for d in range(1, o)]
        for cp in cps:
            cp.start()
        outer_ex.append(cps)

    for c in range(nc):
        for cp in outer_ex[c]:
            cp.wait_recv()

        def finish(r, carry, c=c):
            at = strip(r)
            acc = OWN[c, :, at]
            for d in range(1, o):
                acc = acc + YR[d, c, :, at].astype(F32)
            for v in range(nvar):
                out[v, :, strip(c * cr + r)] = acc[v * lm:(v + 1) * lm]
            return carry

        lax.fori_loop(0, cr, finish, 0)

    for cps in pert_ex + filt_ex + outer_ex:
        for cp in cps:
            cp.wait_send()
    for b, (band, cps) in enumerate(geo_all):
        if b < ng // 2:
            for cp in cps:
                cp.wait_send()
        else:
            @pl.when(band != geo)
            def _(cps=cps):
                for cp in cps:
                    cp.wait_send()


def body(nm, ng, control, kappa_table, kappa_index, tile_bounds, filter_bands, perturbation):
    _, lev, hx, hy = control.shape
    nvar, _, levels, cols = perturbation.shape
    lm = levels // nm
    rows = hx // ng
    tiles, nband, _ = filter_bands.shape
    q = inner_size(nm)
    o = nm // q
    wide = levels // q
    cr = max(1, rows // 4)
    nc = rows // cr
    npc = 1
    cw = cr * hy
    dma = pltpu.SemaphoreType.DMA
    hbm = pl.BlockSpec(memory_space=pl.ANY)
    return pl.pallas_call(
        functools.partial(kernel, nm, ng, q),
        out_shape=jax.ShapeDtypeStruct((nvar, lm, cols), F32),
        in_specs=[hbm] * 6,
        out_specs=pl.BlockSpec(memory_space=pltpu.VMEM),
        scratch_shapes=[
            pltpu.SMEM(kappa_table.shape, F32),
            pltpu.SMEM(tile_bounds.shape, jnp.int32),
            pltpu.VMEM((hx, lev, hy), F32),
            pltpu.VMEM((hx, lev, hy), F32),
            pltpu.VMEM((hx, lev, hy), F32),
            pltpu.VMEM((hx, lev, hy), F32),
            pltpu.VMEM((ITERS, lev, hy), F32),
            pltpu.VMEM((hy, hy), BF16),
            pltpu.VMEM((hy, hy), BF16),
            pltpu.VMEM((hx, hy), jnp.int32),
            pltpu.VMEM((hx + 8, hy), F32),
            pltpu.VMEM((nband, tiles, levels), F32),
            pltpu.VMEM((tiles, nband, levels, LANES), F32),
            pltpu.VMEM((nband, levels, cols), F32),
            pltpu.VMEM((nvar, levels, cols), BF16),
            pltpu.VMEM((q, nc - npc, nvar * wide, cw), BF16),
            pltpu.VMEM((q, nc - npc, nvar * wide, cw), BF16),
            pltpu.VMEM((hx, lev, hy), BF16),
            pltpu.VMEM((ng, rows, lev, hy), BF16),
            pltpu.VMEM((levels + 16, cols), F32),
            pltpu.VMEM((q, nc, wide, cw), BF16),
            pltpu.VMEM((q, nc, wide, cw), BF16),
            pltpu.VMEM((q, npc, nvar * wide, cw), BF16),
            pltpu.VMEM((q, npc, nvar * wide, cw), BF16),
            pltpu.VMEM((nc, nvar * lm, cw), F32),
            pltpu.VMEM((o, nc, nvar * lm, cw), BF16),
            pltpu.VMEM((o, nc, nvar * lm, cw), BF16),
            dma((5 + lev,)), dma((q, nc)), dma((q, nc)), dma((ng, nc)), dma((ng, nc)),
            dma((q, nc)), dma((q, nc)), dma((o, nc)), dma((o, nc)),
        ],
        compiler_params=pltpu.CompilerParams(
            collective_id=0, has_side_effects=True, vmem_limit_bytes=56 * 2**20),
    )(control, kappa_table, kappa_index, tile_bounds, jnp.swapaxes(filter_bands, 0, 1), perturbation)


def solution(mesh):
    in_specs = (P("mem", "geo", None, None), P(), P(), P(), P(), P(None, "mem", None, "geo"))
    out_specs = P(None, "mem", "geo")
    run = functools.partial(body, mesh.shape["mem"], mesh.shape["geo"])
    return jax.shard_map(run, mesh=mesh, in_specs=in_specs, out_specs=out_specs, check_vma=False)
```

profile of v0, /device:TPU:0, one launch (start us, length us, event | category | flops | bytes accessed | tf_op | source)
XLA Modules:
  0.0 26.5 jit_solution(15861242804368757332)
XLA Ops:
  0.0 24.9 %shard_map.64 = f32[2,4,4608]{2,1,0:T(4,128)} custom-call(f32[1,8,48,384]{3,2,1,0:T(8,128)} %ctrl.1, f32[16]{0:T(128)} %table_hbm.1, s32[48,384]{1,0:T(8,128)} %kidx_hbm.1, s32[5]{0:T(128)} %bounds_hbm.1, f32[5,4,32]{2,1,0:T(4,128)} %bitcast.1, bf16[2,1,32,4608]{3,2,1,0:T(8,128)(2,1)} %pert_hbm.1), custom_call_target="tpu_custom_call" | custom-call | tf_op jit(solution)/shard_map/pallas_call | solution.py:357
  25.0 1.6 %copy.8 = f32[2,4,4608]{2,1,0:T(4,128)} copy(f32[2,4,4608]{2,1,0:T(4,128)} %shard_map.64) | data formatting | bytes 294912
where the time goes:
time: 26.7 us; the launch traced here: 26.5 us
  Pallas kernels  24.9 us (93%)
  local copies, waits for them, and re-layouts  1.58 us (6%)
    pallas_call x1, Pallas kernels, body(): pl.pallas_call(functools.partial(kernel, nm, ng, q), out_shape=jax.ShapeD...  24.9 us
    unnamed x1, local copies, waits for them, and re-layouts  1.58 us

commit v1 on v0

--- a/solution.py
+++ b/solution.py
@@ -20,7 +20,7 @@
 
 
 def kernel(nm, ng, q, ctrl, table_hbm, kidx_hbm, bounds_hbm, bands_hbm, pert_hbm, out,
-           table, bounds, C, S, WE, WN, FL, spread, gather, kidx, kf, bands, bandsb, coef, pert,
+           table, bounds, C, S, WE, WN, WS, FL, spread, gather, kidx, kf, bands, bandsb, coef, pert,
            PS, PR, B, G, D, FS, FR, XS, XR, OWN, YS, YR,
            loc_sem, ps_sem, pr_sem, gs_sem, gr_sem, as_sem, ar_sem, bs_sem, br_sem):
     mem = lax.axis_index("mem")
@@ -92,12 +92,14 @@
     norths = [0.5 * (cut[p] + cut[p + 1]) for p in range(parts - 1)]
     last = 0.5 * (cut[-1] + pltpu.roll(cut[0], LANES - 1, axis=1))
     norths.append(jnp.where(lane < LANES - 1, last, 0.0))
+    south = pltpu.roll(norths[-1], 1, axis=1)
     for i in range(hx):
         if i < hx - 1:
             WE[turned(i, hx - 2)] = jnp.broadcast_to(east[i:i + 1], (lev, hy))
         to = turned(i, hx - 1)
         for p in range(parts):
             WN[to, :, p * LANES:(p + 1) * LANES] = jnp.broadcast_to(norths[p][i:i + 1], (lev, LANES))
+        WS[to] = jnp.broadcast_to(south[i:i + 1], (lev, LANES))
 
     def piece(vals, i):
         return jnp.concatenate([v[(k * q + i) * lm:(k * q + i + 1) * lm] for v in vals for k in range(o)], axis=0)
@@ -143,19 +145,18 @@
     def row_of(ref, i):
         return [ref[i, :, p * LANES:(p + 1) * LANES] for p in range(parts)]
 
-    def sweep(it, lo, count, first, final):
+    def sweep(it, lo, hi):
         s = row_of(S, lo)
-        before = None if first else row_of(FL, it)
-        for j in range(count):
-            i = lo + j
+        before = row_of(FL, it) if lo else None
+        for i in range(lo, hi):
             wn = row_of(WN, i)
             ahead = s[1:] + [pltpu.roll(s[0], LANES - 1, axis=1)]
             flux = [wn[p] * (ahead[p] - s[p]) for p in range(parts)]
-            behind = [pltpu.roll(flux[-1], 1, axis=1)] + flux[:-1]
+            behind = [WS[i] * (s[0] - pltpu.roll(s[-1], 1, axis=1))] + flux[:-1]
             new = [s[p] + (flux[p] - behind[p]) for p in range(parts)]
             if before is not None:
                 new = [new[p] - before[p] for p in range(parts)]
-            if not (final and j == count - 1):
+            if i < hx - 1:
                 after = row_of(S, i + 1)
                 we = row_of(WE, i)
                 before = [we[p] * (after[p] - s[p]) for p in range(parts)]
@@ -163,41 +164,42 @@
                 s = after
             for p in range(parts):
                 S[i, :, p * LANES:(p + 1) * LANES] = new[p]
-        if not final:
+        if hi < hx:
             for p in range(parts):
                 FL[it, :, p * LANES:(p + 1) * LANES] = before[p]
 
+    half = ng // 2
+    span = half * rows
     geo_all = []
-    for b in range(ng):
+    for b in range(2):
         for it in range(ITERS):
-            ahead = ITERS - 1 - it
-            lo = 0 if b == 0 else min(hx, rows * b + ahead)
-            hi = min(hx, rows * (b + 1) + ahead)
+            lo, hi = (0, min(hx, span + ITERS - 1 - it)) if b == 0 else (min(hx, span + ITERS - 1 - it), hx)
             if hi > lo:
-                sweep(it, lo, hi - lo, lo == 0, hi == hx)
-        band = turned(b, ng - 1)
-        if (rows * lev) % 8 == 0:
-            x = S[b * rows:(b + 1) * rows].reshape(rows * lev, hy).astype(BF16)
-            x = jnp.dot(x, gather[...], preferred_element_type=F32).reshape(rows, lev, hy).astype(BF16)
+                sweep(it, lo, hi)
+        if (span * lev) % 8 == 0:
+            x = S[b * span:(b + 1) * span].reshape(span * lev, hy).astype(BF16)
+            x = jnp.dot(x, gather[...], preferred_element_type=F32).reshape(span, lev, hy).astype(BF16)
         else:
-            x = [jnp.dot(S[b * rows + r].astype(BF16), gather[...], preferred_element_type=F32).astype(BF16)
-                 for r in range(rows)]
-        for r in range(rows):
-            B[turned(b * rows + r, hx - 1)] = x[r]
-        d = lax.rem(band - geo + ng, ng)
-        cps = [pltpu.make_async_remote_copy(
-            src_ref=B.at[pl.ds(band * rows + c * cr, cr)], dst_ref=G.at[geo, pl.ds(c * cr, cr)],
-            send_sem=gs_sem.at[b, c], recv_sem=gr_sem.at[d, c],
-            device_id={"geo": band}, device_id_type=pl.DeviceIdType.MESH) for c in range(nc)]
-        geo_all.append((band, cps))
-        if b < ng // 2:
-            for cp in cps:
-                cp.start()
-        else:
-            @pl.when(band != geo)
-            def _(cps=cps):
+            x = [jnp.dot(S[b * span + r].astype(BF16), gather[...], preferred_element_type=F32).astype(BF16)
+                 for r in range(span)]
+        for r in range(span):
+            B[turned(b * span + r, hx - 1)] = x[r]
+        for j in range(half):
+            band = j + jnp.where(backward, half, 0) if b == 0 else j + jnp.where(backward, 0, half)
+            d = lax.rem(band - geo + ng, ng)
+            cps = [pltpu.make_async_remote_copy(
+                src_ref=B.at[pl.ds(band * rows + c * cr, cr)], dst_ref=G.at[geo, pl.ds(c * cr, cr)],
+                send_sem=gs_sem.at[b * half + j, c], recv_sem=gr_sem.at[d, c],
+                device_id={"geo": band}, device_id_type=pl.DeviceIdType.MESH) for c in range(nc)]
+            geo_all.append((b, band, cps))
+            if b == 0:
                 for cp in cps:
                     cp.start()
+            else:
+                @pl.when(band != geo)
+                def _(cps=cps):
+                    for cp in cps:
+                        cp.start()
 
     own_geo = [pltpu.make_async_copy(B.at[pl.ds(geo * rows + c * cr, cr)], G.at[geo, pl.ds(c * cr, cr)], gr_sem.at[0, c])
                for c in range(nc)]
@@ -328,8 +330,8 @@
     for cps in pert_ex + filt_ex + outer_ex:
         for cp in cps:
             cp.wait_send()
-    for b, (band, cps) in enumerate(geo_all):
-        if b < ng // 2:
+    for b, band, cps in geo_all:
+        if b == 0:
             for cp in cps:
                 cp.wait_send()
         else:
@@ -366,6 +368,7 @@
             pltpu.VMEM((hx, lev, hy), F32),
             pltpu.VMEM((hx, lev, hy), F32),
             pltpu.VMEM((hx, lev, hy), F32),
+            pltpu.VMEM((hx, lev, LANES), F32),
             pltpu.VMEM((ITERS, lev, hy), F32),
             pltpu.VMEM((hy, hy), BF16),
             pltpu.VMEM((hy, hy), BF16),

time: 26.7 us -> 24.1 us (0.903)
  Pallas kernels: 24.9 us -> 22.4 us
    pallas_call x1, Pallas kernels: 24.9 us -> 22.4 us  [body(): pl.pallas_call(functools.partial(kernel, nm, ng, q), out_shape=jax.ShapeD...]
where the time goes in v1:
time: 24.1 us; the launch traced here: 24 us
  Pallas kernels  22.4 us (93%)
  local copies, waits for them, and re-layouts  1.58 us (7%)
    pallas_call x1, Pallas kernels, body(): pl.pallas_call(functools.partial(kernel, nm, ng, q), out_shape=jax.ShapeD...  22.4 us
    unnamed x1, local copies, waits for them, and re-layouts  1.58 us

profile of v1, /device:TPU:0, one launch (start us, length us, event | category | flops | bytes accessed | tf_op | source)
XLA Modules:
  0.0 24.0 jit_solution(12302034974847370725)
XLA Ops:
  0.0 22.4 %shard_map.64 = f32[2,4,4608]{2,1,0:T(4,128)} custom-call(f32[1,8,48,384]{3,2,1,0:T(8,128)} %ctrl.1, f32[16]{0:T(128)} %table_hbm.1, s32[48,384]{1,0:T(8,128)} %kidx_hbm.1, s32[5]{0:T(128)} %bounds_hbm.1, f32[5,4,32]{2,1,0:T(4,128)} %bitcast.1, bf16[2,1,32,4608]{3,2,1,0:T(8,128)(2,1)} %pert_hbm.1), custom_call_target="tpu_custom_call" | custom-call | tf_op jit(solution)/shard_map/pallas_call | solution.py:359
  22.4 1.6 %copy.8 = f32[2,4,4608]{2,1,0:T(4,128)} copy(f32[2,4,4608]{2,1,0:T(4,128)} %shard_map.64) | data formatting | bytes 294912

commit v2 on v1

--- a/solution.py
+++ b/solution.py
@@ -22,7 +22,7 @@
 def kernel(nm, ng, q, ctrl, table_hbm, kidx_hbm, bounds_hbm, bands_hbm, pert_hbm, out,
            table, bounds, C, S, WE, WN, WS, FL, spread, gather, kidx, kf, bands, bandsb, coef, pert,
            PS, PR, B, G, D, FS, FR, XS, XR, OWN, YS, YR,
-           loc_sem, ps_sem, pr_sem, gs_sem, gr_sem, as_sem, ar_sem, bs_sem, br_sem):
+           loc_sem, send_sem, pr_sem, gr_sem, ar_sem, br_sem):
     mem = lax.axis_index("mem")
     geo = lax.axis_index("geo")
     o = nm // q
@@ -36,7 +36,7 @@
     nband, tiles, _ = bands.shape
     parts = hy // LANES
     pad = nband // 2
-    nc = FS.shape[1]
+    nc = OWN.shape[0]
     cr = rows // nc
     cw = cr * hy
     npc = XS.shape[1]
@@ -54,20 +54,20 @@
     for target in targets:
         pl.semaphore_signal(barrier, inc=1, device_id=target, device_id_type=pl.DeviceIdType.MESH)
 
+    def landed(ref, sem):
+        pltpu.make_async_copy(ref, ref, sem).wait()
+
+    pert_cp = pltpu.make_async_copy(pert_hbm.at[:, 0], pert, loc_sem.at[0])
+    pert_cp.start()
     kidx_cp = pltpu.make_async_copy(kidx_hbm, kidx, loc_sem.at[1])
     kidx_cp.start()
-    table_cp = pltpu.make_async_copy(table_hbm, table, loc_sem.at[3])
+    table_cp = pltpu.make_async_copy(table_hbm, table, loc_sem.at[2])
     table_cp.start()
-    pert_cp = pltpu.make_async_copy(pert_hbm.at[:, 0], pert, loc_sem.at[0])
-    pert_cp.start()
-    ctrl_cps = []
     for l in range(lev):
-        cp = pltpu.make_async_copy(ctrl.at[0, l], C.at[:, l], loc_sem.at[5 + l])
-        cp.start()
-        ctrl_cps.append(cp)
-    bands_cp = pltpu.make_async_copy(bands_hbm, bands, loc_sem.at[2])
+        pltpu.make_async_copy(ctrl.at[0, l], C.at[:, l], loc_sem.at[3]).start()
+    bands_cp = pltpu.make_async_copy(bands_hbm, bands, loc_sem.at[4])
     bands_cp.start()
-    bounds_cp = pltpu.make_async_copy(bounds_hbm, bounds, loc_sem.at[4])
+    bounds_cp = pltpu.make_async_copy(bounds_hbm, bounds, loc_sem.at[5])
     bounds_cp.start()
 
     left = lax.broadcasted_iota(jnp.int32, (hy, hy), 0)
@@ -75,11 +75,39 @@
     spread[...] = jnp.where(left == (right % LANES) * parts + right // LANES, 1.0, 0.0).astype(BF16)
     gather[...] = jnp.where(right == (left % LANES) * parts + left // LANES, 1.0, 0.0).astype(BF16)
 
+    def piece(vals, i):
+        return jnp.concatenate([v[(k * q + i) * lm:(k * q + i + 1) * lm] for v in vals for k in range(o)], axis=0)
+
+    def strip(k):
+        return pl.ds(pl.multiple_of(k * hy, LANES), hy)
+
+    pert_cp.wait()
+    for c in range(npc, nc):
+        def repack(r, carry, c=c):
+            at = strip(c * cr + r)
+            vals = [pert[v, :, at].astype(F32) for v in range(nvar)]
+            for i in range(q):
+                PS[i, c - npc, :, strip(r)] = piece(vals, i).astype(BF16)
+            return carry
+
+        lax.fori_loop(0, cr, repack, 0)
+    pl.semaphore_wait(barrier, len(targets))
+
+    def inner_send(src, dst, k, send, recv):
+        for d in range(1, q):
+            pltpu.make_async_remote_copy(
+                src_ref=src.at[lax.rem(inner + d, q), k], dst_ref=dst.at[d, k], send_sem=send, recv_sem=recv,
+                device_id=at_inner(d), device_id_type=pl.DeviceIdType.MESH).start()
+
+    for k in range(nc - npc):
+        inner_send(PS, PR, k, send_sem.at[0], pr_sem.at[k])
+
     def turned(i, last):
         return jnp.where(backward, last - i, i)
 
     kidx_cp.wait()
     table_cp.wait()
+    landed(C, loc_sem.at[3])
     index = jnp.dot(kidx[...].astype(F32).astype(BF16), spread[...], preferred_element_type=F32)
     field = jnp.zeros(index.shape, F32)
     for entry in range(table.shape[0]):
@@ -101,36 +129,6 @@
             WN[to, :, p * LANES:(p + 1) * LANES] = jnp.broadcast_to(norths[p][i:i + 1], (lev, LANES))
         WS[to] = jnp.broadcast_to(south[i:i + 1], (lev, LANES))
 
-    def piece(vals, i):
-        return jnp.concatenate([v[(k * q + i) * lm:(k * q + i + 1) * lm] for v in vals for k in range(o)], axis=0)
-
-    def strip(k):
-        return pl.ds(pl.multiple_of(k * hy, LANES), hy)
-
-    pert_cp.wait()
-    for c in range(npc, nc):
-        def repack(r, carry, c=c):
-            at = strip(c * cr + r)
-            vals = [pert[v, :, at].astype(F32) for v in range(nvar)]
-            for i in range(q):
-                PS[i, c - npc, :, strip(r)] = piece(vals, i).astype(BF16)
-            return carry
-
-        lax.fori_loop(0, cr, repack, 0)
-    pl.semaphore_wait(barrier, len(targets))
-
-    def inner_copy(src, dst, send, recv, c, k, d):
-        return pltpu.make_async_remote_copy(
-            src_ref=src.at[lax.rem(inner + d, q), k], dst_ref=dst.at[d, k], send_sem=send.at[d, c], recv_sem=recv.at[d, c],
-            device_id=at_inner(d), device_id_type=pl.DeviceIdType.MESH)
-
-    pert_ex = [[inner_copy(PS, PR, ps_sem, pr_sem, c, c - npc, d) for d in range(1, q)] for c in range(npc, nc)]
-    for cps in pert_ex:
-        for cp in cps:
-            cp.start()
-
-    for cp in ctrl_cps:
-        cp.wait()
     group = rows if (rows * lev) % 8 == 0 else hx
     for i in range(0, hx, group):
         x = C[i:i + group].reshape(group * lev, hy)
@@ -170,7 +168,6 @@
 
     half = ng // 2
     span = half * rows
-    geo_all = []
     for b in range(2):
         for it in range(ITERS):
             lo, hi = (0, min(hx, span + ITERS - 1 - it)) if b == 0 else (min(hx, span + ITERS - 1 - it), hx)
@@ -186,12 +183,10 @@
             B[turned(b * span + r, hx - 1)] = x[r]
         for j in range(half):
             band = j + jnp.where(backward, half, 0) if b == 0 else j + jnp.where(backward, 0, half)
-            d = lax.rem(band - geo + ng, ng)
             cps = [pltpu.make_async_remote_copy(
                 src_ref=B.at[pl.ds(band * rows + c * cr, cr)], dst_ref=G.at[geo, pl.ds(c * cr, cr)],
-                send_sem=gs_sem.at[b * half + j, c], recv_sem=gr_sem.at[d, c],
+                send_sem=send_sem.at[1], recv_sem=gr_sem.at[c],
                 device_id={"geo": band}, device_id_type=pl.DeviceIdType.MESH) for c in range(nc)]
-            geo_all.append((b, band, cps))
             if b == 0:
                 for cp in cps:
                     cp.start()
@@ -201,10 +196,8 @@
                     for cp in cps:
                         cp.start()
 
-    own_geo = [pltpu.make_async_copy(B.at[pl.ds(geo * rows + c * cr, cr)], G.at[geo, pl.ds(c * cr, cr)], gr_sem.at[0, c])
-               for c in range(nc)]
-    for cp in own_geo:
-        cp.start()
+    for c in range(nc):
+        pltpu.make_async_copy(B.at[pl.ds(geo * rows + c * cr, cr)], G.at[geo, pl.ds(c * cr, cr)], gr_sem.at[c]).start()
 
     bands_cp.wait()
     bounds_cp.wait()
@@ -239,17 +232,8 @@
             value = value + coef[n, :, at] * D[base + n - pad:base + n - pad + levels, at]
         return value.astype(BF16).astype(F32), at
 
-    def arrived(d, c):
-        return pltpu.make_async_remote_copy(
-            src_ref=B.at[pl.ds(c * cr, cr)], dst_ref=G.at[0, pl.ds(c * cr, cr)],
-            send_sem=gs_sem.at[0, c], recv_sem=gr_sem.at[d, c],
-            device_id={"geo": lax.rem(geo + d, ng)}, device_id_type=pl.DeviceIdType.MESH)
-
-    filt_ex = []
     for c in range(nc):
-        own_geo[c].wait()
-        for d in range(1, ng):
-            arrived(d, c).wait_recv()
+        landed(G.at[:, pl.ds(c * cr, cr)], gr_sem.at[c])
 
         def vertical(r, carry, c=c):
             k = c * cr + r
@@ -262,25 +246,22 @@
                     XS[i, c, :, strip(r)] = piece(vals, i).astype(BF16)
             else:
                 for i in range(q):
-                    FS[i, c, :, strip(r)] = piece([value], i).astype(BF16)
+                    FS[i, c - npc, :, strip(r)] = piece([value], i).astype(BF16)
             return carry
 
         lax.fori_loop(0, cr, vertical, 0)
         if c < npc:
-            cps = [inner_copy(XS, XR, as_sem, ar_sem, c, c, d) for d in range(1, q)]
+            inner_send(XS, XR, c, send_sem.at[2], ar_sem.at[c])
         else:
-            cps = [inner_copy(FS, FR, as_sem, ar_sem, c, c, d) for d in range(1, q)]
-        for cp in cps:
-            cp.start()
-        filt_ex.append(cps)
-
-    outer_ex = []
+            inner_send(FS, FR, c - npc, send_sem.at[3], ar_sem.at[c])
+
+    others = pl.ds(1, q - 1)
     for c in range(nc):
-        for cp in filt_ex[c]:
-            cp.wait_recv()
-        if c >= npc:
-            for cp in pert_ex[c - npc]:
-                cp.wait_recv()
+        if c < npc:
+            landed(XR.at[others, c], ar_sem.at[c])
+        else:
+            landed(FR.at[others, c - npc], ar_sem.at[c])
+            landed(PR.at[others, c - npc], pr_sem.at[c - npc])
 
         def total(r, carry, c=c):
             at = strip(r)
@@ -289,10 +270,10 @@
                 for d in range(1, q):
                     acc = acc + XR[d, c, :, at].astype(F32)
             else:
-                f = FS[inner, c, :, at].astype(F32)
+                f = FS[inner, c - npc, :, at].astype(F32)
                 acc = PS[inner, c - npc, :, at].astype(F32) * jnp.concatenate([f] * nvar, axis=0)
                 for d in range(1, q):
-                    f = FR[d, c, :, at].astype(F32)
+                    f = FR[d, c - npc, :, at].astype(F32)
                     acc = acc + PR[d, c - npc, :, at].astype(F32) * jnp.concatenate([f] * nvar, axis=0)
             shares = [jnp.concatenate([acc[v * wide + k * lm:v * wide + (k + 1) * lm] for v in range(nvar)], axis=0)
                       for k in range(o)]
@@ -305,16 +286,13 @@
             return carry
 
         lax.fori_loop(0, cr, total, 0)
-        cps = [pltpu.make_async_remote_copy(
-            src_ref=YS.at[lax.rem(outer + d, o), c], dst_ref=YR.at[d, c], send_sem=bs_sem.at[d, c], recv_sem=br_sem.at[d, c],
-            device_id=at_outer(d), device_id_type=pl.DeviceIdType.MESH) for d in range(1, o)]
-        for cp in cps:
-            cp.start()
-        outer_ex.append(cps)
+        for d in range(1, o):
+            pltpu.make_async_remote_copy(
+                src_ref=YS.at[lax.rem(outer + d, o), c], dst_ref=YR.at[d, c], send_sem=send_sem.at[4], recv_sem=br_sem.at[c],
+                device_id=at_outer(d), device_id_type=pl.DeviceIdType.MESH).start()
 
     for c in range(nc):
-        for cp in outer_ex[c]:
-            cp.wait_recv()
+        landed(YR.at[pl.ds(1, o - 1), c], br_sem.at[c])
 
         def finish(r, carry, c=c):
             at = strip(r)
@@ -327,18 +305,11 @@
 
         lax.fori_loop(0, cr, finish, 0)
 
-    for cps in pert_ex + filt_ex + outer_ex:
-        for cp in cps:
-            cp.wait_send()
-    for b, band, cps in geo_all:
-        if b == 0:
-            for cp in cps:
-                cp.wait_send()
-        else:
-            @pl.when(band != geo)
-            def _(cps=cps):
-                for cp in cps:
-                    cp.wait_send()
+    landed(PS.at[pl.ds(0, q - 1)], send_sem.at[0])
+    landed(B.at[pl.ds(0, hx - rows)], send_sem.at[1])
+    landed(XS.at[pl.ds(0, q - 1)], send_sem.at[2])
+    landed(FS.at[pl.ds(0, q - 1)], send_sem.at[3])
+    landed(YS.at[pl.ds(0, o - 1)], send_sem.at[4])
 
 
 def body(nm, ng, control, kappa_table, kappa_index, tile_bounds, filter_bands, perturbation):
@@ -358,7 +329,7 @@
     hbm = pl.BlockSpec(memory_space=pl.ANY)
     return pl.pallas_call(
         functools.partial(kernel, nm, ng, q),
-        out_shape=jax.ShapeDtypeStruct((nvar, lm, cols), F32),
+        out_shape=pltpu.VMEM((nvar, lm, cols), F32),
         in_specs=[hbm] * 6,
         out_specs=pl.BlockSpec(memory_space=pltpu.VMEM),
         scratch_shapes=[
@@ -383,15 +354,14 @@
             pltpu.VMEM((hx, lev, hy), BF16),
             pltpu.VMEM((ng, rows, lev, hy), BF16),
             pltpu.VMEM((levels + 16, cols), F32),
-            pltpu.VMEM((q, nc, wide, cw), BF16),
-            pltpu.VMEM((q, nc, wide, cw), BF16),
+            pltpu.VMEM((q, nc - npc, wide, cw), BF16),
+            pltpu.VMEM((q, nc - npc, wide, cw), BF16),
             pltpu.VMEM((q, npc, nvar * wide, cw), BF16),
             pltpu.VMEM((q, npc, nvar * wide, cw), BF16),
             pltpu.VMEM((nc, nvar * lm, cw), F32),
             pltpu.VMEM((o, nc, nvar * lm, cw), BF16),
             pltpu.VMEM((o, nc, nvar * lm, cw), BF16),
-            dma((5 + lev,)), dma((q, nc)), dma((q, nc)), dma((ng, nc)), dma((ng, nc)),
-            dma((q, nc)), dma((q, nc)), dma((o, nc)), dma((o, nc)),
+            dma((6,)), dma((5,)), dma((nc - npc,)), dma((nc,)), dma((nc,)), dma((nc,)),
         ],
         compiler_params=pltpu.CompilerParams(
             collective_id=0, has_side_effects=True, vmem_limit_bytes=56 * 2**20),

time: 24.1 us -> 21.5 us (0.89)
  Pallas kernels: 22.4 us -> 20.7 us
  local copies, waits for them, and re-layouts: 1.58 us -> 0.66 us
    pallas_call x1, Pallas kernels: 22.4 us -> 20.7 us  [body(): pl.pallas_call(functools.partial(kernel, nm, ng, q), out_shape=pltpu.VMEM...]
    unnamed x1, local copies, waits for them, and re-layouts: 1.58 us -> 0.66 us
where the time goes in v2:
time: 21.5 us; the launch traced here: 21.3 us
  Pallas kernels  20.7 us (96%)
  local copies, waits for them, and re-layouts  0.66 us (3%)
    pallas_call x1, Pallas kernels, body(): pl.pallas_call(functools.partial(kernel, nm, ng, q), out_shape=pltpu.VMEM...  20.7 us
    unnamed x1, local copies, waits for them, and re-layouts  0.66 us

profile of v2, /device:TPU:0, one launch (start us, length us, event | category | flops | bytes accessed | tf_op | source)
XLA Modules:
  0.0 21.3 jit_solution(12681637047155655206)
XLA Ops:
  0.0 20.7 %shard_map.64 = f32[2,4,4608]{2,1,0:T(4,128)S(1)} custom-call(f32[1,8,48,384]{3,2,1,0:T(8,128)} %ctrl.1, f32[16]{0:T(128)} %table_hbm.1, s32[48,384]{1,0:T(8,128)} %kidx_hbm.1, s32[5]{0:T(128)} %bounds_hbm.1, f32[5,4,32]{2,1,0:T(4,128)} %bitcast.1, bf16[2,1,32,4608]{3,2,1,0:T(8,128)(2,1)} %pert_hbm.1), custom_call_target="tpu_custom_call" | custom-call | tf_op jit(solution)/shard_map/pallas_call | solution.py:330
  20.7 0.7 %copy.8 = f32[2,4,4608]{2,1,0:T(4,128)} copy(f32[2,4,4608]{2,1,0:T(4,128)S(1)} %shard_map.64) | data formatting | bytes 294912

commit v3 on v2

--- a/solution.py
+++ b/solution.py
@@ -41,6 +41,8 @@
     cw = cr * hy
     npc = XS.shape[1]
     backward = geo < ng // 2
+    near = lax.rem(geo, 2) == 1
+    far = jnp.logical_not(near)
 
     def at_inner(d):
         return {"mem": outer * q + lax.rem(inner + d, q)}
@@ -82,25 +84,38 @@
         return pl.ds(pl.multiple_of(k * hy, LANES), hy)
 
     pert_cp.wait()
-    for c in range(npc, nc):
-        def repack(r, carry, c=c):
+    def repack(c):
+        def step(r, carry):
             at = strip(c * cr + r)
             vals = [pert[v, :, at].astype(F32) for v in range(nvar)]
             for i in range(q):
-                PS[i, c - npc, :, strip(r)] = piece(vals, i).astype(BF16)
+                PS[i, c, :, strip(r)] = piece(vals, i).astype(BF16)
             return carry
 
-        lax.fori_loop(0, cr, repack, 0)
-    pl.semaphore_wait(barrier, len(targets))
-
-    def inner_send(src, dst, k, send, recv):
+        lax.fori_loop(0, cr, step, 0)
+
+    def inner_send(src, dst, c, send, recv):
         for d in range(1, q):
             pltpu.make_async_remote_copy(
-                src_ref=src.at[lax.rem(inner + d, q), k], dst_ref=dst.at[d, k], send_sem=send, recv_sem=recv,
+                src_ref=src.at[lax.rem(inner + d, q), c], dst_ref=dst.at[d, c], send_sem=send, recv_sem=recv,
                 device_id=at_inner(d), device_id_type=pl.DeviceIdType.MESH).start()
 
-    for k in range(nc - npc):
-        inner_send(PS, PR, k, send_sem.at[0], pr_sem.at[k])
+    @pl.when(far)
+    def _():
+        for c in range(npc):
+            repack(c)
+
+    for c in range(npc, nc):
+        repack(c)
+    pl.semaphore_wait(barrier, len(targets))
+
+    @pl.when(far)
+    def _():
+        for c in range(npc):
+            inner_send(PS, PR, c, send_sem.at[5], pr_sem.at[c])
+
+    for c in range(npc, nc):
+        inner_send(PS, PR, c, send_sem.at[0], pr_sem.at[c])
 
     def turned(i, last):
         return jnp.where(backward, last - i, i)
@@ -232,49 +247,56 @@
             value = value + coef[n, :, at] * D[base + n - pad:base + n - pad + levels, at]
         return value.astype(BF16).astype(F32), at
 
-    for c in range(nc):
-        landed(G.at[:, pl.ds(c * cr, cr)], gr_sem.at[c])
-
-        def vertical(r, carry, c=c):
+    def vertical(c, products, send):
+        def step(r, carry):
             k = c * cr + r
             for g in range(ng):
                 D[base + g * lev:base + (g + 1) * lev, strip(k)] = G[g, k].astype(F32)
             value, at = filtered(k)
-            if c < npc:
+            if products:
                 vals = [pert[v, :, at].astype(F32) * value for v in range(nvar)]
                 for i in range(q):
                     XS[i, c, :, strip(r)] = piece(vals, i).astype(BF16)
             else:
                 for i in range(q):
-                    FS[i, c - npc, :, strip(r)] = piece([value], i).astype(BF16)
+                    FS[i, c, :, strip(r)] = piece([value], i).astype(BF16)
             return carry
 
-        lax.fori_loop(0, cr, vertical, 0)
+        lax.fori_loop(0, cr, step, 0)
+        if products:
+            inner_send(XS, XR, c, send, ar_sem.at[c])
+        else:
+            inner_send(FS, FR, c, send, ar_sem.at[c])
+
+    for c in range(nc):
+        landed(G.at[:, pl.ds(c * cr, cr)], gr_sem.at[c])
         if c < npc:
-            inner_send(XS, XR, c, send_sem.at[2], ar_sem.at[c])
+            pl.when(near)(functools.partial(vertical, c, True, send_sem.at[2]))
+            pl.when(far)(functools.partial(vertical, c, False, send_sem.at[6]))
         else:
-            inner_send(FS, FR, c - npc, send_sem.at[3], ar_sem.at[c])
+            vertical(c, False, send_sem.at[3])
 
     others = pl.ds(1, q - 1)
-    for c in range(nc):
-        if c < npc:
+
+    def total(c, products):
+        if products:
             landed(XR.at[others, c], ar_sem.at[c])
         else:
-            landed(FR.at[others, c - npc], ar_sem.at[c])
-            landed(PR.at[others, c - npc], pr_sem.at[c - npc])
-
-        def total(r, carry, c=c):
+            landed(FR.at[others, c], ar_sem.at[c])
+            landed(PR.at[others, c], pr_sem.at[c])
+
+        def step(r, carry):
             at = strip(r)
-            if c < npc:
+            if products:
                 acc = XS[inner, c, :, at].astype(F32)
                 for d in range(1, q):
                     acc = acc + XR[d, c, :, at].astype(F32)
             else:
-                f = FS[inner, c - npc, :, at].astype(F32)
-                acc = PS[inner, c - npc, :, at].astype(F32) * jnp.concatenate([f] * nvar, axis=0)
+                f = FS[inner, c, :, at].astype(F32)
+                acc = PS[inner, c, :, at].astype(F32) * jnp.concatenate([f] * nvar, axis=0)
                 for d in range(1, q):
-                    f = FR[d, c - npc, :, at].astype(F32)
-                    acc = acc + PR[d, c - npc, :, at].astype(F32) * jnp.concatenate([f] * nvar, axis=0)
+                    f = FR[d, c, :, at].astype(F32)
+                    acc = acc + PR[d, c, :, at].astype(F32) * jnp.concatenate([f] * nvar, axis=0)
             shares = [jnp.concatenate([acc[v * wide + k * lm:v * wide + (k + 1) * lm] for v in range(nvar)], axis=0)
                       for k in range(o)]
             mine = shares[0]
@@ -285,7 +307,14 @@
             OWN[c, :, at] = mine
             return carry
 
-        lax.fori_loop(0, cr, total, 0)
+        lax.fori_loop(0, cr, step, 0)
+
+    for c in range(nc):
+        if c < npc:
+            pl.when(near)(functools.partial(total, c, True))
+            pl.when(far)(functools.partial(total, c, False))
+        else:
+            total(c, False)
         for d in range(1, o):
             pltpu.make_async_remote_copy(
                 src_ref=YS.at[lax.rem(outer + d, o), c], dst_ref=YR.at[d, c], send_sem=send_sem.at[4], recv_sem=br_sem.at[c],
@@ -305,11 +334,20 @@
 
         lax.fori_loop(0, cr, finish, 0)
 
-    landed(PS.at[pl.ds(0, q - 1)], send_sem.at[0])
+    peers = pl.ds(0, q - 1)
+    landed(PS.at[peers, pl.ds(npc, nc - npc)], send_sem.at[0])
     landed(B.at[pl.ds(0, hx - rows)], send_sem.at[1])
-    landed(XS.at[pl.ds(0, q - 1)], send_sem.at[2])
-    landed(FS.at[pl.ds(0, q - 1)], send_sem.at[3])
+    landed(FS.at[peers, pl.ds(npc, nc - npc)], send_sem.at[3])
     landed(YS.at[pl.ds(0, o - 1)], send_sem.at[4])
+
+    @pl.when(near)
+    def _():
+        landed(XS.at[peers], send_sem.at[2])
+
+    @pl.when(far)
+    def _():
+        landed(PS.at[peers, pl.ds(0, npc)], send_sem.at[5])
+        landed(FS.at[peers, pl.ds(0, npc)], send_sem.at[6])
 
 
 def body(nm, ng, control, kappa_table, kappa_index, tile_bounds, filter_bands, perturbation):
@@ -323,7 +361,7 @@
     wide = levels // q
     cr = max(1, rows // 4)
     nc = rows // cr
-    npc = 1
+    npc = nc // 2
     cw = cr * hy
     dma = pltpu.SemaphoreType.DMA
     hbm = pl.BlockSpec(memory_space=pl.ANY)
@@ -349,19 +387,19 @@
             pltpu.VMEM((tiles, nband, levels, LANES), F32),
             pltpu.VMEM((nband, levels, cols), F32),
             pltpu.VMEM((nvar, levels, cols), BF16),
-            pltpu.VMEM((q, nc - npc, nvar * wide, cw), BF16),
-            pltpu.VMEM((q, nc - npc, nvar * wide, cw), BF16),
+            pltpu.VMEM((q, nc, nvar * wide, cw), BF16),
+            pltpu.VMEM((q, nc, nvar * wide, cw), BF16),
             pltpu.VMEM((hx, lev, hy), BF16),
             pltpu.VMEM((ng, rows, lev, hy), BF16),
             pltpu.VMEM((levels + 16, cols), F32),
-            pltpu.VMEM((q, nc - npc, wide, cw), BF16),
-            pltpu.VMEM((q, nc - npc, wide, cw), BF16),
+            pltpu.VMEM((q, nc, wide, cw), BF16),
+            pltpu.VMEM((q, nc, wide, cw), BF16),
             pltpu.VMEM((q, npc, nvar * wide, cw), BF16),
             pltpu.VMEM((q, npc, nvar * wide, cw), BF16),
             pltpu.VMEM((nc, nvar * lm, cw), F32),
             pltpu.VMEM((o, nc, nvar * lm, cw), BF16),
             pltpu.VMEM((o, nc, nvar * lm, cw), BF16),
-            dma((6,)), dma((5,)), dma((nc - npc,)), dma((nc,)), dma((nc,)), dma((nc,)),
+            dma((6,)), dma((7,)), dma((nc,)), dma((nc,)), dma((nc,)), dma((nc,)),
         ],
         compiler_params=pltpu.CompilerParams(
             collective_id=0, has_side_effects=True, vmem_limit_bytes=56 * 2**20),

time: 21.5 us -> 20.6 us (0.958)
  the two profiles are of different devices: /device:TPU:0 before, /device:TPU:1 now
where the time goes in v3:
time: 20.6 us; the launch traced here: 20.5 us
  Pallas kernels  19.8 us (96%)
  local copies, waits for them, and re-layouts  0.66 us (3%)
    pallas_call x1, Pallas kernels, body(): pl.pallas_call(functools.partial(kernel, nm, ng, q), out_shape=pltpu.VMEM...  19.8 us
    unnamed x1, local copies, waits for them, and re-layouts  0.66 us

profile of v3, /device:TPU:1, one launch (start us, length us, event | category | flops | bytes accessed | tf_op | source)
XLA Modules:
  0.0 20.5 jit_solution(9484502693997056598)
XLA Ops:
  0.0 19.8 %shard_map.64 = f32[2,4,4608]{2,1,0:T(4,128)S(1)} custom-call(f32[1,8,48,384]{3,2,1,0:T(8,128)} %ctrl.1, f32[16]{0:T(128)} %table_hbm.1, s32[48,384]{1,0:T(8,128)} %kidx_hbm.1, s32[5]{0:T(128)} %bounds_hbm.1, f32[5,4,32]{2,1,0:T(4,128)} %bitcast.1, bf16[2,1,32,4608]{3,2,1,0:T(8,128)(2,1)} %pert_hbm.1), custom_call_target="tpu_custom_call" | custom-call | tf_op jit(solution)/shard_map/pallas_call | solution.py:368
  19.8 0.7 %copy.8 = f32[2,4,4608]{2,1,0:T(4,128)} copy(f32[2,4,4608]{2,1,0:T(4,128)S(1)} %shard_map.64) | data formatting | bytes 294912

commit v4 on v3

--- a/solution.py
+++ b/solution.py
@@ -22,7 +22,7 @@
 def kernel(nm, ng, q, ctrl, table_hbm, kidx_hbm, bounds_hbm, bands_hbm, pert_hbm, out,
            table, bounds, C, S, WE, WN, WS, FL, spread, gather, kidx, kf, bands, bandsb, coef, pert,
            PS, PR, B, G, D, FS, FR, XS, XR, OWN, YS, YR,
-           loc_sem, send_sem, pr_sem, gr_sem, ar_sem, br_sem):
+           loc_sem, pert_sem, send_sem, pr_sem, gr_sem, ar_sem, br_sem):
     mem = lax.axis_index("mem")
     geo = lax.axis_index("geo")
     o = nm // q
@@ -59,8 +59,10 @@
     def landed(ref, sem):
         pltpu.make_async_copy(ref, ref, sem).wait()
 
-    pert_cp = pltpu.make_async_copy(pert_hbm.at[:, 0], pert, loc_sem.at[0])
-    pert_cp.start()
+    pert_cps = [pltpu.make_async_copy(pert_hbm.at[:, 0, :, pl.ds(c * cw, cw)], pert.at[:, :, pl.ds(c * cw, cw)], pert_sem.at[c])
+                for c in range(nc)]
+    for cp in pert_cps:
+        cp.start()
     kidx_cp = pltpu.make_async_copy(kidx_hbm, kidx, loc_sem.at[1])
     kidx_cp.start()
     table_cp = pltpu.make_async_copy(table_hbm, table, loc_sem.at[2])
@@ -83,7 +85,6 @@
     def strip(k):
         return pl.ds(pl.multiple_of(k * hy, LANES), hy)
 
-    pert_cp.wait()
     def repack(c):
         def step(r, carry):
             at = strip(c * cr + r)
@@ -100,22 +101,17 @@
                 src_ref=src.at[lax.rem(inner + d, q), c], dst_ref=dst.at[d, c], send_sem=send, recv_sem=recv,
                 device_id=at_inner(d), device_id_type=pl.DeviceIdType.MESH).start()
 
-    @pl.when(far)
-    def _():
-        for c in range(npc):
-            repack(c)
-
-    for c in range(npc, nc):
+    def offer(c, send):
         repack(c)
+        inner_send(PS, PR, c, send, pr_sem.at[c])
+
     pl.semaphore_wait(barrier, len(targets))
-
-    @pl.when(far)
-    def _():
-        for c in range(npc):
-            inner_send(PS, PR, c, send_sem.at[5], pr_sem.at[c])
-
-    for c in range(npc, nc):
-        inner_send(PS, PR, c, send_sem.at[0], pr_sem.at[c])
+    for c in range(nc):
+        pert_cps[c].wait()
+        if c < npc:
+            pl.when(far)(functools.partial(offer, c, send_sem.at[5]))
+        else:
+            offer(c, send_sem.at[0])
 
     def turned(i, last):
         return jnp.where(backward, last - i, i)
@@ -123,7 +119,15 @@
     kidx_cp.wait()
     table_cp.wait()
     landed(C, loc_sem.at[3])
-    index = jnp.dot(kidx[...].astype(F32).astype(BF16), spread[...], preferred_element_type=F32)
+    x = C[...].reshape(hx * lev, hy)
+    high = x.astype(BF16)
+    low = (x - high.astype(F32)).astype(BF16)
+    x = jnp.concatenate([kidx[...].astype(F32).astype(BF16), high, low], axis=0)
+    x = jnp.dot(x, spread[...], preferred_element_type=F32)
+    index = x[:hx]
+    x = (x[hx:hx + hx * lev] + x[hx + hx * lev:]).reshape(hx, lev, hy)
+    for i in range(hx):
+        S[turned(i, hx - 1)] = x[i]
     field = jnp.zeros(index.shape, F32)
     for entry in range(table.shape[0]):
         field = jnp.where(index == float(entry), table[entry], field)
@@ -143,17 +147,6 @@
         for p in range(parts):
             WN[to, :, p * LANES:(p + 1) * LANES] = jnp.broadcast_to(norths[p][i:i + 1], (lev, LANES))
         WS[to] = jnp.broadcast_to(south[i:i + 1], (lev, LANES))
-
-    group = rows if (rows * lev) % 8 == 0 else hx
-    for i in range(0, hx, group):
-        x = C[i:i + group].reshape(group * lev, hy)
-        high = x.astype(BF16)
-        low = (x - high.astype(F32)).astype(BF16)
-        x = (jnp.dot(high, spread[...], preferred_element_type=F32)
-             + jnp.dot(low, spread[...], preferred_element_type=F32))
-        x = x.reshape(group, lev, hy)
-        for r in range(group):
-            S[turned(i + r, hx - 1)] = x[r]
 
     def row_of(ref, i):
         return [ref[i, :, p * LANES:(p + 1) * LANES] for p in range(parts)]
@@ -359,7 +352,7 @@
     q = inner_size(nm)
     o = nm // q
     wide = levels // q
-    cr = max(1, rows // 4)
+    cr = max(1, rows // 6)
     nc = rows // cr
     npc = nc // 2
     cw = cr * hy
@@ -399,7 +392,7 @@
             pltpu.VMEM((nc, nvar * lm, cw), F32),
             pltpu.VMEM((o, nc, nvar * lm, cw), BF16),
             pltpu.VMEM((o, nc, nvar * lm, cw), BF16),
-            dma((6,)), dma((7,)), dma((nc,)), dma((nc,)), dma((nc,)), dma((nc,)),
+            dma((6,)), dma((nc,)), dma((7,)), dma((nc,)), dma((nc,)), dma((nc,)), dma((nc,)),
         ],
         compiler_params=pltpu.CompilerParams(
             collective_id=0, has_side_effects=True, vmem_limit_bytes=56 * 2**20),

time: 20.6 us -> 20.4 us (level)
  the two profiles are of different devices: /device:TPU:1 before, /device:TPU:0 now
where the time goes in v4:
time: 20.4 us; the launch traced here: 20.1 us
  Pallas kernels  19.5 us (96%)
  local copies, waits for them, and re-layouts  0.66 us (3%)
    pallas_call x1, Pallas kernels, body(): pl.pallas_call(functools.partial(kernel, nm, ng, q), out_shape=pltpu.VMEM...  19.5 us
    unnamed x1, local copies, waits for them, and re-layouts  0.66 us

profile of v4, /device:TPU:0, one launch (start us, length us, event | category | flops | bytes accessed | tf_op | source)
XLA Modules:
  0.0 20.1 jit_solution(7291976416335057065)
XLA Ops:
  0.0 19.5 %shard_map.64 = f32[2,4,4608]{2,1,0:T(4,128)S(1)} custom-call(f32[1,8,48,384]{3,2,1,0:T(8,128)} %ctrl.1, f32[16]{0:T(128)} %table_hbm.1, s32[48,384]{1,0:T(8,128)} %kidx_hbm.1, s32[5]{0:T(128)} %bounds_hbm.1, f32[5,4,32]{2,1,0:T(4,128)} %bitcast.1, bf16[2,1,32,4608]{3,2,1,0:T(8,128)(2,1)} %pert_hbm.1), custom_call_target="tpu_custom_call" | custom-call | tf_op jit(solution)/shard_map/pallas_call | solution.py:361
  19.5 0.7 %copy.8 = f32[2,4,4608]{2,1,0:T(4,128)} copy(f32[2,4,4608]{2,1,0:T(4,128)S(1)} %shard_map.64) | data formatting | bytes 294912

commit v5 on v4

--- a/solution.py
+++ b/solution.py
@@ -21,8 +21,8 @@
 
 def kernel(nm, ng, q, ctrl, table_hbm, kidx_hbm, bounds_hbm, bands_hbm, pert_hbm, out,
            table, bounds, C, S, WE, WN, WS, FL, spread, gather, kidx, kf, bands, bandsb, coef, pert,
-           PS, PR, B, G, D, FS, FR, XS, XR, OWN, YS, YR,
-           loc_sem, pert_sem, send_sem, pr_sem, gr_sem, ar_sem, br_sem):
+           PS, PR, B, G, D, FS, FR, XS, XR, YS, YR,
+           loc_sem, pert_sem, send_sem, pr_sem, gr_sem, ar_sem, zr_sem, br_sem):
     mem = lax.axis_index("mem")
     geo = lax.axis_index("geo")
     o = nm // q
@@ -31,12 +31,11 @@
     hx, lev, hy = S.shape
     nvar, levels, cols = pert.shape
     lm = levels // nm
-    wide = levels // q
     rows = hx // ng
     nband, tiles, _ = bands.shape
     parts = hy // LANES
     pad = nband // 2
-    nc = OWN.shape[0]
+    nc = YS.shape[1]
     cr = rows // nc
     cw = cr * hy
     npc = XS.shape[1]
@@ -63,24 +62,25 @@
                 for c in range(nc)]
     for cp in pert_cps:
         cp.start()
-    kidx_cp = pltpu.make_async_copy(kidx_hbm, kidx, loc_sem.at[1])
+    kidx_cp = pltpu.make_async_copy(kidx_hbm, kidx, loc_sem.at[0])
     kidx_cp.start()
-    table_cp = pltpu.make_async_copy(table_hbm, table, loc_sem.at[2])
+    table_cp = pltpu.make_async_copy(table_hbm, table, loc_sem.at[1])
     table_cp.start()
     for l in range(lev):
-        pltpu.make_async_copy(ctrl.at[0, l], C.at[:, l], loc_sem.at[3]).start()
-    bands_cp = pltpu.make_async_copy(bands_hbm, bands, loc_sem.at[4])
-    bands_cp.start()
-    bounds_cp = pltpu.make_async_copy(bounds_hbm, bounds, loc_sem.at[5])
-    bounds_cp.start()
-
+        pltpu.make_async_copy(ctrl.at[0, l], C.at[:, l], loc_sem.at[2]).start()
     left = lax.broadcasted_iota(jnp.int32, (hy, hy), 0)
     right = lax.broadcasted_iota(jnp.int32, (hy, hy), 1)
     spread[...] = jnp.where(left == (right % LANES) * parts + right // LANES, 1.0, 0.0).astype(BF16)
     gather[...] = jnp.where(right == (left % LANES) * parts + left // LANES, 1.0, 0.0).astype(BF16)
 
-    def piece(vals, i):
-        return jnp.concatenate([v[(k * q + i) * lm:(k * q + i + 1) * lm] for v in vals for k in range(o)], axis=0)
+    def piece(vals, i, k):
+        return jnp.concatenate([v[(k * q + i) * lm:(k * q + i + 1) * lm] for v in vals], axis=0)
+
+    def split(ref, vals, c, at):
+        for k in range(o):
+            slot = lax.rem(k - outer + o, o)
+            for i in range(q):
+                ref[i, c, slot, :, at] = piece(vals, i, k).astype(BF16)
 
     def strip(k):
         return pl.ds(pl.multiple_of(k * hy, LANES), hy)
@@ -89,36 +89,39 @@
         def step(r, carry):
             at = strip(c * cr + r)
             vals = [pert[v, :, at].astype(F32) for v in range(nvar)]
-            for i in range(q):
-                PS[i, c, :, strip(r)] = piece(vals, i).astype(BF16)
+            split(PS, vals, c, strip(r))
             return carry
 
         lax.fori_loop(0, cr, step, 0)
 
-    def inner_send(src, dst, c, send, recv):
+    crossing = pl.ds(1, o - 1)
+    whole = pl.ds(0, o)
+    staying = pl.ds(0, 1)
+
+    def inner_send(src, dst, c, part, send, recv):
         for d in range(1, q):
             pltpu.make_async_remote_copy(
-                src_ref=src.at[lax.rem(inner + d, q), c], dst_ref=dst.at[d, c], send_sem=send, recv_sem=recv,
+                src_ref=src.at[lax.rem(inner + d, q), c, part], dst_ref=dst.at[d, c, part], send_sem=send, recv_sem=recv,
                 device_id=at_inner(d), device_id_type=pl.DeviceIdType.MESH).start()
 
-    def offer(c, send):
+    def offer(c):
         repack(c)
-        inner_send(PS, PR, c, send, pr_sem.at[c])
+        inner_send(PS, PR, c, whole, send_sem.at[0], pr_sem.at[0 if c >= npc else 1])
 
     pl.semaphore_wait(barrier, len(targets))
     for c in range(nc):
         pert_cps[c].wait()
         if c < npc:
-            pl.when(far)(functools.partial(offer, c, send_sem.at[5]))
-        else:
-            offer(c, send_sem.at[0])
+            pl.when(far)(functools.partial(offer, c))
+        else:
+            offer(c)
 
     def turned(i, last):
         return jnp.where(backward, last - i, i)
 
     kidx_cp.wait()
     table_cp.wait()
-    landed(C, loc_sem.at[3])
+    landed(C, loc_sem.at[2])
     x = C[...].reshape(hx * lev, hy)
     high = x.astype(BF16)
     low = (x - high.astype(F32)).astype(BF16)
@@ -148,6 +151,11 @@
             WN[to, :, p * LANES:(p + 1) * LANES] = jnp.broadcast_to(norths[p][i:i + 1], (lev, LANES))
         WS[to] = jnp.broadcast_to(south[i:i + 1], (lev, LANES))
 
+    bands_cp = pltpu.make_async_copy(bands_hbm, bands, loc_sem.at[0])
+    bands_cp.start()
+    bounds_cp = pltpu.make_async_copy(bounds_hbm, bounds, loc_sem.at[1])
+    bounds_cp.start()
+
     def row_of(ref, i):
         return [ref[i, :, p * LANES:(p + 1) * LANES] for p in range(parts)]
 
@@ -240,7 +248,7 @@
             value = value + coef[n, :, at] * D[base + n - pad:base + n - pad + levels, at]
         return value.astype(BF16).astype(F32), at
 
-    def vertical(c, products, send):
+    def vertical(c, products):
         def step(r, carry):
             k = c * cr + r
             for g in range(ng):
@@ -248,99 +256,116 @@
             value, at = filtered(k)
             if products:
                 vals = [pert[v, :, at].astype(F32) * value for v in range(nvar)]
-                for i in range(q):
-                    XS[i, c, :, strip(r)] = piece(vals, i).astype(BF16)
+                split(XS, vals, c, strip(r))
             else:
-                for i in range(q):
-                    FS[i, c, :, strip(r)] = piece([value], i).astype(BF16)
+                split(FS, [value], c, strip(r))
             return carry
 
         lax.fori_loop(0, cr, step, 0)
+
+    def hand(c, products, part, send, recv):
         if products:
-            inner_send(XS, XR, c, send, ar_sem.at[c])
-        else:
-            inner_send(FS, FR, c, send, ar_sem.at[c])
+            inner_send(XS, XR, c, part, send, recv.at[c])
+        else:
+            inner_send(FS, FR, c, part, send, recv.at[c])
+
+    def vertical_send(c, products, send):
+        vertical(c, products)
+        hand(c, products, crossing, send, ar_sem)
 
     for c in range(nc):
         landed(G.at[:, pl.ds(c * cr, cr)], gr_sem.at[c])
         if c < npc:
-            pl.when(near)(functools.partial(vertical, c, True, send_sem.at[2]))
-            pl.when(far)(functools.partial(vertical, c, False, send_sem.at[6]))
-        else:
-            vertical(c, False, send_sem.at[3])
+            pl.when(near)(functools.partial(vertical_send, c, True, send_sem.at[2]))
+            pl.when(far)(functools.partial(vertical_send, c, False, send_sem.at[3]))
+        else:
+            vertical_send(c, False, send_sem.at[3])
+
+    def later(c):
+        if c < npc:
+            pl.when(near)(functools.partial(hand, c, True, staying, send_sem.at[2], zr_sem))
+            pl.when(far)(functools.partial(hand, c, False, staying, send_sem.at[3], zr_sem))
+        else:
+            hand(c, False, staying, send_sem.at[3], zr_sem)
 
     others = pl.ds(1, q - 1)
 
-    def total(c, products):
+    def summed(c, k, at, products):
         if products:
-            landed(XR.at[others, c], ar_sem.at[c])
-        else:
-            landed(FR.at[others, c], ar_sem.at[c])
-            landed(PR.at[others, c], pr_sem.at[c])
+            acc = XS[inner, c, k, :, at].astype(F32)
+            for d in range(1, q):
+                acc = acc + XR[d, c, k, :, at].astype(F32)
+        else:
+            f = FS[inner, c, k, :, at].astype(F32)
+            acc = PS[inner, c, k, :, at].astype(F32) * jnp.concatenate([f] * nvar, axis=0)
+            for d in range(1, q):
+                f = FR[d, c, k, :, at].astype(F32)
+                acc = acc + PR[d, c, k, :, at].astype(F32) * jnp.concatenate([f] * nvar, axis=0)
+        return acc
+
+    def cross(c, products):
+        landed((XR if products else FR).at[others, c, crossing], ar_sem.at[c])
+        if not products and c == 0:
+            landed(PR.at[others, pl.ds(0, npc)], pr_sem.at[1])
+        if c == npc:
+            landed(PR.at[others, pl.ds(npc, nc - npc)], pr_sem.at[0])
 
         def step(r, carry):
             at = strip(r)
-            if products:
-                acc = XS[inner, c, :, at].astype(F32)
-                for d in range(1, q):
-                    acc = acc + XR[d, c, :, at].astype(F32)
-            else:
-                f = FS[inner, c, :, at].astype(F32)
-                acc = PS[inner, c, :, at].astype(F32) * jnp.concatenate([f] * nvar, axis=0)
-                for d in range(1, q):
-                    f = FR[d, c, :, at].astype(F32)
-                    acc = acc + PR[d, c, :, at].astype(F32) * jnp.concatenate([f] * nvar, axis=0)
-            shares = [jnp.concatenate([acc[v * wide + k * lm:v * wide + (k + 1) * lm] for v in range(nvar)], axis=0)
-                      for k in range(o)]
-            mine = shares[0]
-            for k in range(o):
-                YS[k, c, :, at] = shares[k].astype(BF16)
-                if k:
-                    mine = jnp.where(outer == k, shares[k], mine)
-            OWN[c, :, at] = mine
+            for k in range(1, o):
+                YS[k, c, :, at] = summed(c, k, at, products).astype(BF16)
             return carry
 
         lax.fori_loop(0, cr, step, 0)
-
-    for c in range(nc):
-        if c < npc:
-            pl.when(near)(functools.partial(total, c, True))
-            pl.when(far)(functools.partial(total, c, False))
-        else:
-            total(c, False)
-        for d in range(1, o):
+        for k in range(1, o):
             pltpu.make_async_remote_copy(
-                src_ref=YS.at[lax.rem(outer + d, o), c], dst_ref=YR.at[d, c], send_sem=send_sem.at[4], recv_sem=br_sem.at[c],
-                device_id=at_outer(d), device_id_type=pl.DeviceIdType.MESH).start()
-
-    for c in range(nc):
-        landed(YR.at[pl.ds(1, o - 1), c], br_sem.at[c])
-
-        def finish(r, carry, c=c):
+                src_ref=YS.at[k, c], dst_ref=YR.at[k, c], send_sem=send_sem.at[4], recv_sem=br_sem.at[c],
+                device_id=at_outer(k), device_id_type=pl.DeviceIdType.MESH).start()
+
+    def finish(c, products):
+        landed((XR if products else FR).at[others, c, staying], zr_sem.at[c])
+        landed(YR.at[crossing, c], br_sem.at[c])
+
+        def step(r, carry):
             at = strip(r)
-            acc = OWN[c, :, at]
-            for d in range(1, o):
-                acc = acc + YR[d, c, :, at].astype(F32)
+            acc = summed(c, 0, at, products)
+            for k in range(1, o):
+                acc = acc + YR[k, c, :, at].astype(F32)
             for v in range(nvar):
                 out[v, :, strip(c * cr + r)] = acc[v * lm:(v + 1) * lm]
             return carry
 
-        lax.fori_loop(0, cr, finish, 0)
+        lax.fori_loop(0, cr, step, 0)
+
+    def each(act, c):
+        if c < npc:
+            pl.when(near)(functools.partial(act, c, True))
+            pl.when(far)(functools.partial(act, c, False))
+        else:
+            act(c, False)
+
+    each(cross, 0)
+    for c in range(nc):
+        later(c)
+    for c in range(1, nc):
+        each(cross, c)
+    for c in range(nc):
+        each(finish, c)
 
     peers = pl.ds(0, q - 1)
-    landed(PS.at[peers, pl.ds(npc, nc - npc)], send_sem.at[0])
     landed(B.at[pl.ds(0, hx - rows)], send_sem.at[1])
-    landed(FS.at[peers, pl.ds(npc, nc - npc)], send_sem.at[3])
-    landed(YS.at[pl.ds(0, o - 1)], send_sem.at[4])
+    landed(YS.at[crossing], send_sem.at[4])
 
     @pl.when(near)
     def _():
+        landed(PS.at[peers, pl.ds(npc, nc - npc)], send_sem.at[0])
         landed(XS.at[peers], send_sem.at[2])
+        landed(FS.at[peers, pl.ds(npc, nc - npc)], send_sem.at[3])
 
     @pl.when(far)
     def _():
-        landed(PS.at[peers, pl.ds(0, npc)], send_sem.at[5])
-        landed(FS.at[peers, pl.ds(0, npc)], send_sem.at[6])
+        landed(PS.at[peers], send_sem.at[0])
+        landed(FS.at[peers], send_sem.at[3])
 
 
 def body(nm, ng, control, kappa_table, kappa_index, tile_bounds, filter_bands, perturbation):
@@ -351,10 +376,9 @@
     tiles, nband, _ = filter_bands.shape
     q = inner_size(nm)
     o = nm // q
-    wide = levels // q
     cr = max(1, rows // 6)
     nc = rows // cr
-    npc = nc // 2
+    npc = 1
     cw = cr * hy
     dma = pltpu.SemaphoreType.DMA
     hbm = pl.BlockSpec(memory_space=pl.ANY)
@@ -380,19 +404,18 @@
             pltpu.VMEM((tiles, nband, levels, LANES), F32),
             pltpu.VMEM((nband, levels, cols), F32),
             pltpu.VMEM((nvar, levels, cols), BF16),
-            pltpu.VMEM((q, nc, nvar * wide, cw), BF16),
-            pltpu.VMEM((q, nc, nvar * wide, cw), BF16),
+            pltpu.VMEM((q, nc, o, nvar * lm, cw), BF16),
+            pltpu.VMEM((q, nc, o, nvar * lm, cw), BF16),
             pltpu.VMEM((hx, lev, hy), BF16),
             pltpu.VMEM((ng, rows, lev, hy), BF16),
             pltpu.VMEM((levels + 16, cols), F32),
-            pltpu.VMEM((q, nc, wide, cw), BF16),
-            pltpu.VMEM((q, nc, wide, cw), BF16),
-            pltpu.VMEM((q, npc, nvar * wide, cw), BF16),
-            pltpu.VMEM((q, npc, nvar * wide, cw), BF16),
-            pltpu.VMEM((nc, nvar * lm, cw), F32),
+            pltpu.VMEM((q, nc, o, lm, cw), BF16),
+            pltpu.VMEM((q, nc, o, lm, cw), BF16),
+            pltpu.VMEM((q, npc, o, nvar * lm, cw), BF16),
+            pltpu.VMEM((q, npc, o, nvar * lm, cw), BF16),
             pltpu.VMEM((o, nc, nvar * lm, cw), BF16),
             pltpu.VMEM((o, nc, nvar * lm, cw), BF16),
-            dma((6,)), dma((nc,)), dma((7,)), dma((nc,)), dma((nc,)), dma((nc,)), dma((nc,)),
+            dma((3,)), dma((nc,)), dma((5,)), dma((2,)), dma((nc,)), dma((nc,)), dma((nc,)), dma((nc,)),
         ],
         compiler_params=pltpu.CompilerParams(
             collective_id=0, has_side_effects=True, vmem_limit_bytes=56 * 2**20),

time: 20.4 us -> 19.9 us (0.975)
  Pallas kernels: 19.5 us -> 19.1 us
    pallas_call x1, Pallas kernels: 19.5 us -> 19.1 us  [body(): pl.pallas_call(functools.partial(kernel, nm, ng, q), out_shape=pltpu.VMEM...]
where the time goes in v5:
time: 19.9 us; the launch traced here: 19.8 us
  Pallas kernels  19.1 us (96%)
  local copies, waits for them, and re-layouts  0.66 us (3%)
    pallas_call x1, Pallas kernels, body(): pl.pallas_call(functools.partial(kernel, nm, ng, q), out_shape=pltpu.VMEM...  19.1 us
    unnamed x1, local copies, waits for them, and re-layouts  0.66 us

profile of v5, /device:TPU:0, one launch (start us, length us, event | category | flops | bytes accessed | tf_op | source)
XLA Modules:
  0.0 19.8 jit_solution(13055324133529753294)
XLA Ops:
  0.0 19.1 %shard_map.64 = f32[2,4,4608]{2,1,0:T(4,128)S(1)} custom-call(f32[1,8,48,384]{3,2,1,0:T(8,128)} %ctrl.1, f32[16]{0:T(128)} %table_hbm.1, s32[48,384]{1,0:T(8,128)} %kidx_hbm.1, s32[5]{0:T(128)} %bounds_hbm.1, f32[5,4,32]{2,1,0:T(4,128)} %bitcast.1, bf16[2,1,32,4608]{3,2,1,0:T(8,128)(2,1)} %pert_hbm.1), custom_call_target="tpu_custom_call" | custom-call | tf_op jit(solution)/shard_map/pallas_call | solution.py:385
  19.1 0.7 %copy.8 = f32[2,4,4608]{2,1,0:T(4,128)} copy(f32[2,4,4608]{2,1,0:T(4,128)S(1)} %shard_map.64) | data formatting | bytes 294912

commit v6 on v5

--- a/solution.py
+++ b/solution.py
@@ -344,11 +344,10 @@
         else:
             act(c, False)
 
-    each(cross, 0)
     for c in range(nc):
-        later(c)
-    for c in range(1, nc):
         each(cross, c)
+        for e in range(2 * c, min(nc, 2 * c + 2)):
+            later(e)
     for c in range(nc):
         each(finish, c)
 

time: 19.9 us -> 19.8 us (level)
  no operation moved by 1% of the time
where the time goes in v6:
time: 19.8 us; the launch traced here: 19.6 us
  Pallas kernels  19 us (96%)
  local copies, waits for them, and re-layouts  0.66 us (3%)
    pallas_call x1, Pallas kernels, body(): pl.pallas_call(functools.partial(kernel, nm, ng, q), out_shape=pltpu.VMEM...  19 us
    unnamed x1, local copies, waits for them, and re-layouts  0.66 us

profile of v6, /device:TPU:0, one launch (start us, length us, event | category | flops | bytes accessed | tf_op | source)
XLA Modules:
  0.0 19.6 jit_solution(4326240384779252488)
XLA Ops:
  0.0 19.0 %shard_map.64 = f32[2,4,4608]{2,1,0:T(4,128)S(1)} custom-call(f32[1,8,48,384]{3,2,1,0:T(8,128)} %ctrl.1, f32[16]{0:T(128)} %table_hbm.1, s32[48,384]{1,0:T(8,128)} %kidx_hbm.1, s32[5]{0:T(128)} %bounds_hbm.1, f32[5,4,32]{2,1,0:T(4,128)} %bitcast.1, bf16[2,1,32,4608]{3,2,1,0:T(8,128)(2,1)} %pert_hbm.1), custom_call_target="tpu_custom_call" | custom-call | tf_op jit(solution)/shard_map/pallas_call | solution.py:384
  19.0 0.7 %copy.8 = f32[2,4,4608]{2,1,0:T(4,128)} copy(f32[2,4,4608]{2,1,0:T(4,128)S(1)} %shard_map.64) | data formatting | bytes 294912

commit v7 on v6

--- a/solution.py
+++ b/solution.py
@@ -22,7 +22,7 @@
 def kernel(nm, ng, q, ctrl, table_hbm, kidx_hbm, bounds_hbm, bands_hbm, pert_hbm, out,
            table, bounds, C, S, WE, WN, WS, FL, spread, gather, kidx, kf, bands, bandsb, coef, pert,
            PS, PR, B, G, D, FS, FR, XS, XR, YS, YR,
-           loc_sem, pert_sem, send_sem, pr_sem, gr_sem, ar_sem, zr_sem, br_sem):
+           loc_sem, pert_sem, send_sem, pr_sem, gr_sem, ar_sem, br_sem):
     mem = lax.axis_index("mem")
     geo = lax.axis_index("geo")
     o = nm // q
@@ -283,10 +283,10 @@
 
     def later(c):
         if c < npc:
-            pl.when(near)(functools.partial(hand, c, True, staying, send_sem.at[2], zr_sem))
-            pl.when(far)(functools.partial(hand, c, False, staying, send_sem.at[3], zr_sem))
-        else:
-            hand(c, False, staying, send_sem.at[3], zr_sem)
+            pl.when(near)(functools.partial(hand, c, True, staying, send_sem.at[2], pert_sem))
+            pl.when(far)(functools.partial(hand, c, False, staying, send_sem.at[3], pert_sem))
+        else:
+            hand(c, False, staying, send_sem.at[3], pert_sem)
 
     others = pl.ds(1, q - 1)
 
@@ -323,7 +323,7 @@
                 device_id=at_outer(k), device_id_type=pl.DeviceIdType.MESH).start()
 
     def finish(c, products):
-        landed((XR if products else FR).at[others, c, staying], zr_sem.at[c])
+        landed((XR if products else FR).at[others, c, staying], pert_sem.at[c])
         landed(YR.at[crossing, c], br_sem.at[c])
 
         def step(r, carry):
@@ -414,7 +414,7 @@
             pltpu.VMEM((q, npc, o, nvar * lm, cw), BF16),
             pltpu.VMEM((o, nc, nvar * lm, cw), BF16),
             pltpu.VMEM((o, nc, nvar * lm, cw), BF16),
-            dma((3,)), dma((nc,)), dma((5,)), dma((2,)), dma((nc,)), dma((nc,)), dma((nc,)), dma((nc,)),
+            dma((3,)), dma((nc,)), dma((5,)), dma((2,)), dma((nc,)), dma((nc,)), dma((nc,)),
         ],
         compiler_params=pltpu.CompilerParams(
             collective_id=0, has_side_effects=True, vmem_limit_bytes=56 * 2**20),

time: 19.8 us -> 19.7 us (level)
  no operation moved by 1% of the time
where the time goes in v7:
time: 19.7 us; the launch traced here: 19.6 us
  Pallas kernels  18.9 us (96%)
  local copies, waits for them, and re-layouts  0.66 us (3%)
    pallas_call x1, Pallas kernels, body(): pl.pallas_call(functools.partial(kernel, nm, ng, q), out_shape=pltpu.VMEM...  18.9 us
    unnamed x1, local copies, waits for them, and re-layouts  0.66 us

profile of v7, /device:TPU:0, one launch (start us, length us, event | category | flops | bytes accessed | tf_op | source)
XLA Modules:
  0.0 19.6 jit_solution(12480312718171555497)
XLA Ops:
  0.0 18.9 %shard_map.64 = f32[2,4,4608]{2,1,0:T(4,128)S(1)} custom-call(f32[1,8,48,384]{3,2,1,0:T(8,128)} %ctrl.1, f32[16]{0:T(128)} %table_hbm.1, s32[48,384]{1,0:T(8,128)} %kidx_hbm.1, s32[5]{0:T(128)} %bounds_hbm.1, f32[5,4,32]{2,1,0:T(4,128)} %bitcast.1, bf16[2,1,32,4608]{3,2,1,0:T(8,128)(2,1)} %pert_hbm.1), custom_call_target="tpu_custom_call" | custom-call | tf_op jit(solution)/shard_map/pallas_call | solution.py:384
  18.9 0.7 %copy.8 = f32[2,4,4608]{2,1,0:T(4,128)} copy(f32[2,4,4608]{2,1,0:T(4,128)S(1)} %shard_map.64) | data formatting | bytes 294912
